TPU v7x, 32 devices: a whole 2x2x4 slice. The times are simulated.
32 devices in a mesh: grp: 4 (over y, core), rows: 8 (over z, x).
Axes of the slice: x: 2, y: 2, z: 4, core: 2. Of those that a mesh axis runs over, the one named last changes fastest.
Arguments:
- rhs: float32 [2048, 64, 128], P(('grp', 'rows')), may hold values from -6 to 6
- fine_diag: bfloat16 [2048, 64, 64], P(('grp', 'rows')), may hold values from -0.2 to 1.2
- fine_smoother: bfloat16 [2048, 64, 64], P(('grp', 'rows')), may hold values from -4 to 4
- fine_blocks: bfloat16 [2048, 7, 64, 64], P(('grp', 'rows')), may hold values from -0.1796875 to 0.1796875
- fine_cols: int32 [2048, 7], P(('grp', 'rows')), may hold values from 0 to 2047, as said below
- aggregate: int32 [2048], P(('grp', 'rows')), may hold values from 0 to 511, as said below
- coarse_diag: bfloat16 [512, 64, 64], P('rows'), may hold values from -0.8 to 4.8
- coarse_smoother: bfloat16 [512, 64, 64], P('rows'), may hold values from -1 to 1
- coarse_blocks: bfloat16 [512, 7, 64, 64], P('rows'), may hold values from -0.71875 to 0.71875
- coarse_cols: int32 [512, 7], P('rows'), may hold values from 0 to 511, as said below
Outputs:
- solution: float32 [2048, 64, 128], P(('grp', 'rows'))
Inputs may be any that keep to these rules, and one draw needn't show every extreme that they name: fine_cols row i names rows within 32 of i; the distance 32 is reached. coarse_cols row c names rows within 32 of c; the distance 32 is reached. `aggregate`: aggregate_i lies in [r * 64, (r + 1) * 64) with r = (i // 64) mod 8.
All inputs are finite; a program needn't handle non-finite values.
Results may differ from a plain program's by a relative error of at most 0.001.
The roundings to bfloat16 on the way count: a program that leaves them out, or rounds other values in their place, can miss the bound.
Values may be sent and summed in bfloat16 or wider, within the bound.
A program may use at most 128 MiB of HBM per device.

v0:
```python
import jax
import jax.numpy as jnp
from jax import lax
from jax.sharding import PartitionSpec as P

damping = 0.8


def extended_2(cells, sides, width):
    for axis, dim in sides:
        count = lax.axis_size(axis)
        ends = count - 1
        head = lax.slice_in_dim(cells, 0, width, axis=dim)
        tail = lax.slice_in_dim(cells, cells.shape[dim] - width, cells.shape[dim], axis=dim)
        cells = jnp.concatenate(
            [
                lax.ppermute(tail, axis, [(i, (i + 1) % count) for i in range(ends)]),
                cells,
                lax.ppermute(head, axis, [((i + 1) % count, i) for i in range(ends)]),
            ],
            axis=dim,
        )
    return cells


def block_product(blocks, vector):
    return jnp.einsum(
        "nab,nbk->nak", blocks, vector.astype(jnp.bfloat16), preferred_element_type=jnp.float32
    )


def nearby_product(off_blocks, columns, extended, first_row):
    nearby = jnp.take(extended, columns - first_row, axis=0)
    return jnp.einsum("njab,njbk->nak", off_blocks, nearby, preferred_element_type=jnp.float32)


def fine_operator(fine_diag, fine_blocks, fine_cols, vector):
    rounded_rows = vector.astype(jnp.bfloat16)
    height = vector.shape[0]
    margin = height // 2
    extended = extended_2(rounded_rows, ((("grp", "rows"), 0),), margin)
    first_row = lax.axis_index(("grp", "rows")) * height - margin
    return block_product(fine_diag, rounded_rows) + nearby_product(
        fine_blocks, fine_cols, extended, first_row
    )


def coarse_nearby(off_blocks, columns, rounded_full):
    height = rounded_full.shape[0]
    margin = height // 2
    extended = extended_2(rounded_full, (("rows", 0),), margin)
    first_row = lax.axis_index("rows") * height - margin
    return nearby_product(off_blocks, columns, extended, first_row)


def on_device(
    rhs,
    fine_diag,
    fine_smoother,
    fine_blocks,
    fine_cols,
    aggregate,
    coarse_diag,
    coarse_smoother,
    coarse_blocks,
    coarse_cols,
):
    first_iterate = damping * block_product(fine_smoother, rhs)
    first_residual = rhs - fine_operator(fine_diag, fine_blocks, fine_cols, first_iterate)
    second_iterate = first_iterate + damping * block_product(fine_smoother, first_residual)
    second_residual = rhs - fine_operator(fine_diag, fine_blocks, fine_cols, second_iterate)
    coarse_height = coarse_diag.shape[0]
    local_index = aggregate - lax.axis_index("rows") * coarse_height
    selector = (local_index[:, None] == jnp.arange(coarse_height, dtype=jnp.int32)[None, :]).astype(
        jnp.float32
    )
    partial_sum = jnp.einsum(
        "fc,fak->cak", selector, second_residual, precision=lax.Precision.HIGHEST
    )
    coarse_rhs = lax.psum(partial_sum, "grp")
    coarse_first = damping * block_product(coarse_smoother, coarse_rhs)
    rounded_first = coarse_first.astype(jnp.bfloat16)
    coarse_image = block_product(coarse_diag, rounded_first) + coarse_nearby(
        coarse_blocks, coarse_cols, rounded_first
    )
    coarse_second = coarse_first + damping * block_product(
        coarse_smoother, coarse_rhs - coarse_image
    )
    return second_iterate + jnp.take(coarse_second, local_index, axis=0)


def solution(mesh):
    in_specs = (
        P(("grp", "rows"), None, None),
        P(("grp", "rows"), None, None),
        P(("grp", "rows"), None, None),
        P(("grp", "rows"), None, None, None),
        P(("grp", "rows"), None),
        P(("grp", "rows")),
        P("rows", None, None),
        P("rows", None, None),
        P("rows", None, None, None),
        P("rows", None),
    )
    out_specs = P(("grp", "rows"), None, None)
    return jax.shard_map(
        on_device, mesh=mesh, in_specs=in_specs, out_specs=out_specs, check_vma=False
    )
```

profile of v0, /device:TPU:0, one launch (start us, length us, event | category | flops | bytes accessed | tf_op | source)
XLA Modules:
  0.0 246.3 jit_solution(17737860054501911996)
XLA Ops:
  7.8 3.4 %multiply_convert_fusion.1 = (bf16[64,64,128]{2,1,0:T(8,128)(2,1)S(1)}, f32[64,64,128]{2,1,0:T(8,128)}) fusion(bf16[64,64,64]{2,1,0:T(8,128)(2,1)S(1)} %copy-done, f32[64,64,128]{2,1,0:T(8,128)} %param.12), kind=kOutput, calls=%fused_computation.33 | convolution fusion | flops 68681728 | bytes 5767168 | tf_op jit(solution)/shard_map/nab,nbk->nak/dot_general | solution.py:27
  13.6 6.3 %collective-permute-start = (bf16[32,64,128]{2,1,0:T(8,128)(2,1)}, bf16[32,64,128]{2,1,0:T(8,128)(2,1)}, u32[]{:S(2)}, u32[]{:S(2)}) collective-permute-start(bf16[32,64,128]{2,1,0:T(8,128)(2,1)} %get-tuple-element.16), channel_id=1, source_target_pairs={{0,1},{1,2},{2,3},{3,4},{4,5},{5,6},{6,7},{7,8},{8,9},{9,10},{10,1... | collective-permute-start | bytes 1572872 | tf_op jit(solution)/shard_map/ppermute | solution.py:17
  20.3 1.8 fusion.43
  22.1 18.5 %collective-permute-done.1 = bf16[32,64,128]{2,1,0:T(8,128)(2,1)} collective-permute-done((bf16[32,64,128]{2,1,0:T(8,128)(2,1)}, bf16[32,64,128]{2,1,0:T(8,128)(2,1)}, u32[]{:S(2)}, u32[]{:S(2)}) %collective-permute-start.1) | collective-permute-done | bytes 524320 | tf_op jit(solution)/shard_map/ppermute | solution.py:19
  42.4 13.3 %gather_fusion.1 = bf16[448,64,128]{2,1,0:T(8,128)(2,1)} fusion(bf16[128,64,128]{2,1,0:T(8,128)(2,1)S(1)} %pad_maximum_fusion, s32[1024]{0:T(1024)S(1)} %pad_clamp_fusion.2), kind=kCustom, calls=%fused_computation.clone | custom fusion | bytes 14681856 | tf_op jit(solution)/shard_map/jit(_take)/gather | solution.py:33
  55.8 10.1 %fusion.40 = (bf16[64,64,128]{2,1,0:T(8,128)(2,1)S(1)}, f32[64,64,128]{2,1,0:T(8,128)}) fusion(bf16[64,64,64]{2,1,0:T(8,128)(2,1)S(1)} %copy-done, f32[64,64,128]{2,1,0:T(8,128)} %param.12, f32[64,128,64]{1,2,0:T(8,128)} %fusion.43, bf16[64,7,64,64]{3,2,1,0:T(8,128)(2,1)} %param.15, bf16[64,7,64,128]{3,2,1,0:T(8,128)(2,1)} %bitcast.56, ...), kind=kOutput, calls=%fused_computation.61 | convolution fusion | flops 544210944 | bytes 20971968 | tf_op jit(solution)/shard_map/nab,nbk->nak/dot_general | solution.py:27
  67.4 5.2 %collective-permute-start.2 = (bf16[32,64,128]{2,1,0:T(8,128)(2,1)S(1)}, bf16[32,64,128]{2,1,0:T(8,128)(2,1)S(1)}, u32[]{:S(2)}, u32[]{:S(2)}) collective-permute-start(bf16[32,64,128]{2,1,0:T(8,128)(2,1)S(1)} %get-tuple-element.14), channel_id=1, source_target_pairs={{0,1},{1,2},{2,3},{3,4},{4,5},{5,6},{6,7},{7,8},{8,9},{9,10},{10,1... | collective-permute-start | bytes 1572872 | tf_op jit(solution)/shard_map/ppermute | solution.py:17
  72.7 1.8 fusion.44
  74.5 19.4 %collective-permute-done.3 = bf16[32,64,128]{2,1,0:T(8,128)(2,1)S(1)} collective-permute-done((bf16[32,64,128]{2,1,0:T(8,128)(2,1)S(1)}, bf16[32,64,128]{2,1,0:T(8,128)(2,1)S(1)}, u32[]{:S(2)}, u32[]{:S(2)}) %collective-permute-start.3) | collective-permute-done | bytes 524320 | tf_op jit(solution)/shard_map/ppermute | solution.py:19
  95.5 13.3 %gather_fusion.2 = bf16[448,64,128]{2,1,0:T(8,128)(2,1)} fusion(bf16[128,64,128]{2,1,0:T(8,128)(2,1)S(1)} %pad_maximum_fusion.1, s32[1024]{0:T(1024)S(1)} %pad_clamp_fusion.2), kind=kCustom, calls=%fused_computation.1.clone | custom fusion | bytes 14681856 | tf_op jit(solution)/shard_map/jit(_take)/gather | solution.py:33
  108.9 9.2 %bitcast_subtract_fusion.1 = f32[64,64,128]{2,1,0:T(8,128)S(1)} fusion(f32[64,64,128]{2,1,0:T(8,128)} %param.12, f32[64,128,64]{1,2,0:T(8,128)} %fusion.44, bf16[64,7,64,64]{3,2,1,0:T(8,128)(2,1)} %param.15, bf16[64,7,64,128]{3,2,1,0:T(8,128)(2,1)} %bitcast.57, pred[64,7]{1,0:T(8,128)(4,1)S(1)} %copy.17), kind=kOutput, calls=%fused_computation.22 | convolution fusion | flops 474480640 | bytes 17301952 | tf_op jit(solution)/shard_map/njab,njbk->nak/dot_general | solution.py:34
  118.1 3.8 %fusion.14 = f32[64,64,128]{2,0,1:T(8,128)} fusion(f32[64,64,128]{2,1,0:T(8,128)S(1)} %bitcast_subtract_fusion.1, s32[64]{0:T(128)S(1)} %get-tuple-element.7), kind=kOutput, calls=%fused_computation.28 | convolution fusion | flops 402657280 | bytes 4194560 | tf_op jit(solution)/shard_map/fc,fak->cak/dot_general | solution.py:77
  122.8 51.9 %all-reduce.2.cloned.1.call-done = f32[64,64,128]{2,0,1:T(8,128)} async-done(((f32[64,64,128]{2,0,1:T(8,128)}), f32[64,64,128]{2,0,1:T(8,128)}) %all-reduce.2.cloned.1.call-update) | async-done | bytes 2097168 | tf_op jit(solution)/shard_map/psum | solution.py:80
  176.5 2.3 fusion.23
  182.0 5.3 %collective-permute-start.4 = (bf16[32,64,128]{2,1,0:T(8,128)(2,1)}, bf16[32,64,128]{2,1,0:T(8,128)(2,1)}, u32[]{:S(2)}, u32[]{:S(2)}) collective-permute-start(bf16[32,64,128]{2,1,0:T(8,128)(2,1)} %get-tuple-element.12), channel_id=1, source_target_pairs={{0,1},{1,2},{2,3},{3,4},{4,5},{5,6},{6,7},{8,9},{9,10},{10,11},{11... | collective-permute-start | bytes 1572872 | tf_op jit(solution)/shard_map/ppermute | solution.py:17
  187.5 3.1 %fusion.28 = f32[64,128,64]{1,2,0:T(8,128)} fusion(bf16[64,64,64]{2,1,0:T(8,128)(2,1)} %param.18, f32[64,128,64]{1,2,0:T(8,128)S(1)} %fusion.23), kind=kOutput, calls=%fused_computation.40 | convolution fusion | flops 68157440 | bytes 4718592 | tf_op jit(solution)/shard_map/nab,nbk->nak/dot_general | solution.py:27
  190.6 5.6 %collective-permute-done.5 = bf16[32,64,128]{2,1,0:T(8,128)(2,1)} collective-permute-done((bf16[32,64,128]{2,1,0:T(8,128)(2,1)}, bf16[32,64,128]{2,1,0:T(8,128)(2,1)}, u32[]{:S(2)}, u32[]{:S(2)}) %collective-permute-start.5) | collective-permute-done | bytes 524320 | tf_op jit(solution)/shard_map/ppermute | solution.py:19
  196.1 11.1 %collective-permute-done.4 = bf16[32,64,128]{2,1,0:T(8,128)(2,1)} collective-permute-done((bf16[32,64,128]{2,1,0:T(8,128)(2,1)}, bf16[32,64,128]{2,1,0:T(8,128)(2,1)}, u32[]{:S(2)}, u32[]{:S(2)}) %collective-permute-start.4) | collective-permute-done | bytes 524320 | tf_op jit(solution)/shard_map/ppermute | solution.py:17
  208.7 13.3 %gather_fusion.3 = bf16[448,64,128]{2,1,0:T(8,128)(2,1)} fusion(bf16[128,64,128]{2,1,0:T(8,128)(2,1)S(1)} %pad_maximum_fusion.2, s32[1024]{0:T(1024)S(1)} %pad_clamp_fusion.1), kind=kCustom, calls=%fused_computation.2.clone | custom fusion | bytes 14681856 | tf_op jit(solution)/shard_map/jit(_take)/gather | solution.py:33
  222.1 6.8 %fusion = f32[64,128,64,1]{1,2,3,0:T(8,128)S(1)} fusion(bf16[64,7,64,64]{3,2,1,0:T(8,128)(2,1)} %param.20, bf16[64,7,64,128]{3,2,1,0:T(8,128)(2,1)} %bitcast.58, pred[64,7]{1,0:T(8,128)(4,1)S(1)} %copy.23), kind=kOutput, calls=%fused_computation.4 | convolution fusion | flops 473432064 | bytes 13107648 | tf_op jit(solution)/shard_map/njab,njbk->nak/dot_general | solution.py:34
  228.9 2.4 fusion.12
  231.3 2.6 %add_bitcast_fusion = f32[64,64,128]{2,1,0:T(8,128)} fusion(f32[64,128,64]{1,2,0:T(8,128)S(1)} %copy-done.3, bf16[64,64,64]{2,1,0:T(8,128)(2,1)S(1)} %copy-done.10, bf16[64,64,128]{2,0,1:T(8,128)(2,1)S(1)} %fusion.12), kind=kOutput, calls=%fused_computation.31 | convolution fusion | flops 68681728 | bytes 5767168 | tf_op jit(solution)/shard_map/nab,nbk->nak/dot_general | solution.py:27
  233.9 2.3 gather_fusion
  236.2 3.3 %select_add_fusion = f32[64,64,128]{2,1,0:T(8,128)} fusion(f32[64,64,128]{2,1,0:T(8,128)} %get-tuple-element.21, f32[64,64,128]{2,1,0:T(8,128)S(1)} %gather_fusion, pred[64]{0:T(512)(128)(4,1)S(1)} %get-tuple-element.6), kind=kLoop, calls=%fused_computation.30 | loop fusion | flops 1048576 | bytes 6291520 | tf_op jit(solution)/shard_map/add | solution.py:89
  (56 shorter events, 16.5 us)
Async XLA Ops:
  6.5 1.2 copy-start
  6.5 168.2 %all-reduce.2.cloned.1.call-start = ((), (), s32[]{:S(2)}) async-start(), calls=%async_computation | async-start | bytes 4194304 | tf_op jit(solution)/shard_map/psum | solution.py:80
  11.1 11.0 %copy-start.4 = (bf16[64,64,128]{2,1,0:T(8,128)(2,1)}, bf16[64,64,128]{2,1,0:T(8,128)(2,1)S(1)}, u32[]{:S(2)}) copy-start(bf16[64,64,128]{2,1,0:T(8,128)(2,1)S(1)} %get-tuple-element.18) | copy-start | bytes 3145732
  11.1 8.8 %copy-start.11 = (s32[64,7]{0,1:T(8,128)S(1)}, s32[64,7]{0,1:T(8,128)}, u32[]{:S(2)}) copy-start(s32[64,7]{0,1:T(8,128)} %param.16) | copy-start | bytes 5380
  11.1 9.1 %copy-start.8 = (bf16[64,64,64]{2,1,0:T(8,128)(2,1)S(1)}, bf16[64,64,64]{2,1,0:T(8,128)(2,1)}, u32[]{:S(2)}) copy-start(bf16[64,64,64]{2,1,0:T(8,128)(2,1)} %param.13) | copy-start | bytes 1572868
  12.2 28.5 %collective-permute-start.1 = (bf16[32,64,128]{2,1,0:T(8,128)(2,1)}, bf16[32,64,128]{2,1,0:T(8,128)(2,1)}, u32[]{:S(2)}, u32[]{:S(2)}) collective-permute-start(bf16[32,64,128]{2,1,0:T(8,128)(2,1)} %get-tuple-element.17), channel_id=1, source_target_pairs={{1,0},{2,1},{3,2},{4,3},{5,4},{6,5},{7,6},{8,7},{9,8},{10,9},{11,1... | collective-permute-start | bytes 1572872 | tf_op jit(solution)/shard_map/ppermute | solution.py:19
  13.6 27.1 %collective-permute-start = (bf16[32,64,128]{2,1,0:T(8,128)(2,1)}, bf16[32,64,128]{2,1,0:T(8,128)(2,1)}, u32[]{:S(2)}, u32[]{:S(2)}) collective-permute-start(bf16[32,64,128]{2,1,0:T(8,128)(2,1)} %get-tuple-element.16), channel_id=1, source_target_pairs={{0,1},{1,2},{2,3},{3,4},{4,5},{5,6},{6,7},{7,8},{8,9},{9,10},{10,1... | collective-permute-start | bytes 1572872 | tf_op jit(solution)/shard_map/ppermute | solution.py:17
  65.9 8.6 %copy-start.5 = (bf16[64,64,128]{2,1,0:T(8,128)(2,1)}, bf16[64,64,128]{2,1,0:T(8,128)(2,1)S(1)}, u32[]{:S(2)}) copy-start(bf16[64,64,128]{2,1,0:T(8,128)(2,1)S(1)} %get-tuple-element.20) | copy-start | bytes 3145732
  65.9 6.8 %copy-start.13 = (s32[64]{0:T(128)S(1)}, s32[64]{0:T(128)}, u32[]{:S(2)}) copy-start(s32[64]{0:T(128)} %param.17) | copy-start | bytes 772
  65.9 6.8 %copy-start.9 = (bf16[64,64,64]{2,1,0:T(8,128)(2,1)S(1)}, bf16[64,64,64]{2,1,0:T(8,128)(2,1)}, u32[]{:S(2)}) copy-start(bf16[64,64,64]{2,1,0:T(8,128)(2,1)} %param.13) | copy-start | bytes 1572868
  65.9 28.0 %collective-permute-start.3 = (bf16[32,64,128]{2,1,0:T(8,128)(2,1)S(1)}, bf16[32,64,128]{2,1,0:T(8,128)(2,1)S(1)}, u32[]{:S(2)}, u32[]{:S(2)}) collective-permute-start(bf16[32,64,128]{2,1,0:T(8,128)(2,1)S(1)} %get-tuple-element.15), channel_id=1, source_target_pairs={{1,0},{2,1},{3,2},{4,3},{5,4},{6,5},{7,6},{8,7},{9,8},{10,9},{11,1... | collective-permute-start | bytes 1572872 | tf_op jit(solution)/shard_map/ppermute | solution.py:19
  67.4 26.7 %collective-permute-start.2 = (bf16[32,64,128]{2,1,0:T(8,128)(2,1)S(1)}, bf16[32,64,128]{2,1,0:T(8,128)(2,1)S(1)}, u32[]{:S(2)}, u32[]{:S(2)}) collective-permute-start(bf16[32,64,128]{2,1,0:T(8,128)(2,1)S(1)} %get-tuple-element.14), channel_id=1, source_target_pairs={{0,1},{1,2},{2,3},{3,4},{4,5},{5,6},{6,7},{7,8},{8,9},{9,10},{10,1... | collective-permute-start | bytes 1572872 | tf_op jit(solution)/shard_map/ppermute | solution.py:17
  121.9 0.7 copy-start.12
  178.8 8.7 %copy-start.2 = (f32[64,128,64]{1,2,0:T(8,128)}, f32[64,128,64]{1,2,0:T(8,128)S(1)}, u32[]{:S(2)}) copy-start(f32[64,128,64]{1,2,0:T(8,128)S(1)} %fusion.23) | copy-start | bytes 6291460
  180.5 15.6 %collective-permute-start.5 = (bf16[32,64,128]{2,1,0:T(8,128)(2,1)}, bf16[32,64,128]{2,1,0:T(8,128)(2,1)}, u32[]{:S(2)}, u32[]{:S(2)}) collective-permute-start(bf16[32,64,128]{2,1,0:T(8,128)(2,1)} %get-tuple-element.13), channel_id=1, source_target_pairs={{1,0},{2,1},{3,2},{4,3},{5,4},{6,5},{7,6},{9,8},{10,9},{11,10},{12... | collective-permute-start | bytes 1572872 | tf_op jit(solution)/shard_map/ppermute | solution.py:19
  182.0 25.2 %collective-permute-start.4 = (bf16[32,64,128]{2,1,0:T(8,128)(2,1)}, bf16[32,64,128]{2,1,0:T(8,128)(2,1)}, u32[]{:S(2)}, u32[]{:S(2)}) collective-permute-start(bf16[32,64,128]{2,1,0:T(8,128)(2,1)} %get-tuple-element.12), channel_id=1, source_target_pairs={{0,1},{1,2},{2,3},{3,4},{4,5},{5,6},{6,7},{8,9},{9,10},{10,11},{11... | collective-permute-start | bytes 1572872 | tf_op jit(solution)/shard_map/ppermute | solution.py:17
  222.0 6.9 %copy-start.6 = (f32[64,64,128]{2,0,1:T(8,128)S(1)}, f32[64,64,128]{2,0,1:T(8,128)}, u32[]{:S(2)}) copy-start(f32[64,64,128]{2,0,1:T(8,128)} %all-reduce.2.cloned.1.call-done) | copy-start | bytes 6291460
  222.0 6.9 %copy-start.7 = (f32[64,128,64]{1,2,0:T(8,128)S(1)}, f32[64,128,64]{1,2,0:T(8,128)}, u32[]{:S(2)}) copy-start(f32[64,128,64]{1,2,0:T(8,128)} %fusion.28) | copy-start | bytes 6291460
  228.9 2.4 copy-start.3
  228.9 2.4 copy-start.10
  236.2 3.3 %copy-start.1 = (bf16[64,64,64]{2,1,0:T(8,128)(2,1)S(1)}, bf16[64,64,64]{2,1,0:T(8,128)(2,1)}, u32[]{:S(2)}) copy-start(bf16[64,64,64]{2,1,0:T(8,128)(2,1)} %param.14) | copy-start | bytes 1572868
Sparse Core Ops, SparseCore 0:
  122.0 52.6 all-reduce.1
where the time goes:
time: 247 us; the launch traced here: 246 us
  waiting for transfers between devices  107 us (43%)
  local copies, waits for them, and re-layouts  47.4 us (19%)
  matrix products  44.8 us (18%)
  starting transfers between devices  21.2 us (9%)
  between operations  13.7 us (6%)
  other arithmetic  12.4 us (5%)
    psum x1, waiting for transfers between devices, on_device(): coarse_rhs = lax.psum(partial_sum, 'grp')  51.9 us
    ppermute x3, waiting for transfers between devices, extended_2(): lax.ppermute(head, axis, [((i + 1) % count, i) for i in range(ends)])  43.5 us
    gather x3, local copies, waits for them, and re-layouts, nearby_product(): nearby = jnp.take(extended, columns - first_row, axis=0)  40 us
    dot_general x7, matrix products, block_product(): jnp.einsum('nab,nbk->nak', blocks, vector.astype(jnp.bfloat16), preferred...  25 us
    ppermute x3, starting transfers between devices, extended_2(): lax.ppermute(tail, axis, [(i, (i + 1) % count) for i in range(ends)])  16.9 us
    dot_general x2, matrix products, nearby_product(): jnp.einsum('njab,njbk->nak', off_blocks, nearby, preferred_element_type=j...  16 us
    ppermute x3, waiting for transfers between devices, extended_2(): lax.ppermute(tail, axis, [(i, (i + 1) % count) for i in range(ends)])  11.4 us
  transfers between devices with their start and end apart: 7, of which 7 were waited for; matrix products, arithmetic and copies ran while one was open for 3% of the time, Pallas kernels for 0%

commit v1 on v0

--- a/solution.py
+++ b/solution.py
@@ -77,7 +77,8 @@
     partial_sum = jnp.einsum(
         "fc,fak->cak", selector, second_residual, precision=lax.Precision.HIGHEST
     )
-    coarse_rhs = lax.psum(partial_sum, "grp")
+    out_arr = lax.all_gather(partial_sum, axis_name="grp")
+    coarse_rhs = jnp.sum(out_arr, axis=0)
     coarse_first = damping * block_product(coarse_smoother, coarse_rhs)
     rounded_first = coarse_first.astype(jnp.bfloat16)
     coarse_image = block_product(coarse_diag, rounded_first) + coarse_nearby(

time: 247 us -> 257 us (1.040)
  waiting for transfers between devices: 107 us -> 119 us
  starting transfers between devices: 21.2 us -> 15.6 us
  local copies, waits for them, and re-layouts: 47.4 us -> 50.2 us
    all_gather x0 -> x1, waiting for transfers between devices: none -> 56.6 us  [on_device(): out_arr = lax.all_gather(partial_sum, axis_name='grp')]
    psum x1 -> x0, waiting for transfers between devices: 51.9 us -> none  [on_device(): coarse_rhs = lax.psum(partial_sum, 'grp')]
    ppermute x3, waiting for transfers between devices: 11.4 us -> 55.6 us  [extended_2(): lax.ppermute(tail, axis, [(i, (i + 1) % count) for i in range(ends)])]
    ppermute x3, waiting for transfers between devices: 43.5 us -> 6.74 us  [extended_2(): lax.ppermute(head, axis, [((i + 1) % count, i) for i in range(ends)])]
    dot_general x2 -> x1, matrix products: 16 us -> 9.17 us  [nearby_product(): jnp.einsum('njab,njbk->nak', off_blocks, nearby, preferred_element_type=j...]
    dot_general x7, matrix products: 25 us -> 31.6 us  [block_product(): jnp.einsum('nab,nbk->nak', blocks, vector.astype(jnp.bfloat16), preferred...]
    ppermute x3, starting transfers between devices: 16.9 us -> 11.5 us  [extended_2(): lax.ppermute(tail, axis, [(i, (i + 1) % count) for i in range(ends)])]
    reduce_sum x0 -> x1, other arithmetic: none -> 4.64 us  [on_device(): coarse_rhs = jnp.sum(out_arr, axis=0)]
  transfers between devices with their start and end apart: 7 -> 7, of which waited for: 7 -> 6; matrix products, arithmetic and copies ran while one was open for 3% -> 3% of each run, Pallas kernels for 0% -> 0%
where the time goes in v1:
time: 257 us; the launch traced here: 256 us
  waiting for transfers between devices  119 us (46%)
  local copies, waits for them, and re-layouts  50.2 us (20%)
  matrix products  44.6 us (17%)
  starting transfers between devices  15.6 us (6%)
  between operations  13.6 us (5%)
  other arithmetic  13.1 us (5%)
    all_gather x1, waiting for transfers between devices, on_device(): out_arr = lax.all_gather(partial_sum, axis_name='grp')  56.6 us
    ppermute x3, waiting for transfers between devices, extended_2(): lax.ppermute(tail, axis, [(i, (i + 1) % count) for i in range(ends)])  55.6 us
    gather x3, local copies, waits for them, and re-layouts, nearby_product(): nearby = jnp.take(extended, columns - first_row, axis=0)  40.5 us
    dot_general x7, matrix products, block_product(): jnp.einsum('nab,nbk->nak', blocks, vector.astype(jnp.bfloat16), preferred...  31.6 us
    ppermute x3, starting transfers between devices, extended_2(): lax.ppermute(tail, axis, [(i, (i + 1) % count) for i in range(ends)])  11.5 us
    dot_general x1, matrix products, nearby_product(): jnp.einsum('njab,njbk->nak', off_blocks, nearby, preferred_element_type=j...  9.17 us
    ppermute x3, waiting for transfers between devices, extended_2(): lax.ppermute(head, axis, [((i + 1) % count, i) for i in range(ends)])  6.74 us
  transfers between devices with their start and end apart: 7, of which 6 were waited for; matrix products, arithmetic and copies ran while one was open for 3% of the time, Pallas kernels for 0%

profile of v1, /device:TPU:0, one launch (start us, length us, event | category | flops | bytes accessed | tf_op | source)
XLA Modules:
  0.0 256.1 jit_solution(5148456155343866585)
XLA Ops:
  7.8 3.4 %multiply_convert_fusion.1 = (bf16[64,64,128]{2,1,0:T(8,128)(2,1)S(1)}, f32[64,64,128]{2,1,0:T(8,128)}) fusion(bf16[64,64,64]{2,1,0:T(8,128)(2,1)S(1)} %copy-done, f32[64,64,128]{2,1,0:T(8,128)} %param.12), kind=kOutput, calls=%fused_computation.33 | convolution fusion | flops 68681728 | bytes 5767168 | tf_op jit(solution)/shard_map/nab,nbk->nak/dot_general | solution.py:27
  12.2 5.8 %collective-permute-start = (bf16[32,64,128]{2,1,0:T(8,128)(2,1)}, bf16[32,64,128]{2,1,0:T(8,128)(2,1)}, u32[]{:S(2)}, u32[]{:S(2)}) collective-permute-start(bf16[32,64,128]{2,1,0:T(8,128)(2,1)} %get-tuple-element.16), channel_id=1, source_target_pairs={{0,1},{1,2},{2,3},{3,4},{4,5},{5,6},{6,7},{7,8},{8,9},{9,10},{10,1... | collective-permute-start | bytes 1572872 | tf_op jit(solution)/shard_map/ppermute | solution.py:17
  19.6 1.8 fusion.47
  21.5 18.4 %collective-permute-done = bf16[32,64,128]{2,1,0:T(8,128)(2,1)} collective-permute-done((bf16[32,64,128]{2,1,0:T(8,128)(2,1)}, bf16[32,64,128]{2,1,0:T(8,128)(2,1)}, u32[]{:S(2)}, u32[]{:S(2)}) %collective-permute-start) | collective-permute-done | bytes 524320 | tf_op jit(solution)/shard_map/ppermute | solution.py:17
  39.9 4.1 %collective-permute-done.1 = bf16[32,64,128]{2,1,0:T(8,128)(2,1)} collective-permute-done((bf16[32,64,128]{2,1,0:T(8,128)(2,1)}, bf16[32,64,128]{2,1,0:T(8,128)(2,1)}, u32[]{:S(2)}, u32[]{:S(2)}) %collective-permute-start.1) | collective-permute-done | bytes 524320 | tf_op jit(solution)/shard_map/ppermute | solution.py:19
  44.0 1.8 pad_maximum_fusion
  45.7 13.3 %gather_fusion.1 = bf16[448,64,128]{2,1,0:T(8,128)(2,1)} fusion(bf16[128,64,128]{2,1,0:T(8,128)(2,1)S(1)} %pad_maximum_fusion, s32[1024]{0:T(1024)S(1)} %pad_clamp_fusion.2), kind=kCustom, calls=%fused_computation.clone | custom fusion | bytes 14681856 | tf_op jit(solution)/shard_map/jit(_take)/gather | solution.py:33
  59.1 10.1 %fusion.44 = (bf16[64,64,128]{2,1,0:T(8,128)(2,1)S(1)}, f32[64,64,128]{2,1,0:T(8,128)}) fusion(bf16[64,64,64]{2,1,0:T(8,128)(2,1)S(1)} %copy-done, f32[64,64,128]{2,1,0:T(8,128)} %param.12, f32[64,128,64]{1,2,0:T(8,128)} %fusion.47, bf16[64,7,64,64]{3,2,1,0:T(8,128)(2,1)} %param.15, bf16[64,7,64,128]{3,2,1,0:T(8,128)(2,1)} %bitcast.63, ...), kind=kOutput, calls=%fused_computation.60 | convolution fusion | flops 544210944 | bytes 20971968 | tf_op jit(solution)/shard_map/nab,nbk->nak/dot_general | solution.py:27
  69.2 1.6 collective-permute-start.2
  72.4 1.8 fusion.48
  74.2 19.4 %collective-permute-done.2 = bf16[32,64,128]{2,1,0:T(8,128)(2,1)S(1)} collective-permute-done((bf16[32,64,128]{2,1,0:T(8,128)(2,1)S(1)}, bf16[32,64,128]{2,1,0:T(8,128)(2,1)S(1)}, u32[]{:S(2)}, u32[]{:S(2)}) %collective-permute-start.2) | collective-permute-done | bytes 524320 | tf_op jit(solution)/shard_map/ppermute | solution.py:17
  93.6 2.6 %collective-permute-done.3 = bf16[32,64,128]{2,1,0:T(8,128)(2,1)S(1)} collective-permute-done((bf16[32,64,128]{2,1,0:T(8,128)(2,1)S(1)}, bf16[32,64,128]{2,1,0:T(8,128)(2,1)S(1)}, u32[]{:S(2)}, u32[]{:S(2)}) %collective-permute-start.3) | collective-permute-done | bytes 524320 | tf_op jit(solution)/shard_map/ppermute | solution.py:19
  97.7 13.6 %gather_fusion.2 = bf16[448,64,128]{2,1,0:T(8,128)(2,1)} fusion(bf16[128,64,128]{2,1,0:T(8,128)(2,1)S(1)} %pad_maximum_fusion.1, s32[1024]{0:T(1024)S(1)} %pad_clamp_fusion.2), kind=kCustom, calls=%fused_computation.1.clone | custom fusion | bytes 14681856 | tf_op jit(solution)/shard_map/jit(_take)/gather | solution.py:33
  111.3 9.2 %bitcast_subtract_fusion.1 = f32[64,64,128]{2,1,0:T(8,128)S(1)} fusion(f32[64,64,128]{2,1,0:T(8,128)} %param.12, f32[64,128,64]{1,2,0:T(8,128)} %fusion.48, bf16[64,7,64,64]{3,2,1,0:T(8,128)(2,1)} %param.15, bf16[64,7,64,128]{3,2,1,0:T(8,128)(2,1)} %bitcast.65, pred[64,7]{1,0:T(8,128)(4,1)S(1)} %copy.22), kind=kOutput, calls=%fused_computation.22 | convolution fusion | flops 474480640 | bytes 17301952 | tf_op jit(solution)/shard_map/njab,njbk->nak/dot_general | solution.py:34
  120.5 3.9 %fusion.14 = f32[64,64,128]{2,0,1:T(8,128)} fusion(f32[64,64,128]{2,1,0:T(8,128)S(1)} %bitcast_subtract_fusion.1, s32[64]{0:T(128)S(1)} %get-tuple-element.7), kind=kOutput, calls=%fused_computation.28 | convolution fusion | flops 402657280 | bytes 4194560 | tf_op jit(solution)/shard_map/fc,fak->cak/dot_general | solution.py:77
  125.3 56.6 %all-gather.3.cloned.1.call-done = f32[256,64,128]{2,0,1:T(8,128)} async-done(((f32[64,64,128]{2,0,1:T(8,128)}), f32[256,64,128]{2,0,1:T(8,128)}) %all-gather.3.cloned.1.call-update) | async-done | bytes 8388624 | tf_op jit(solution)/shard_map/all_gather | solution.py:80
  181.9 4.6 %reduce_sum.9 = f32[64,64,128]{2,0,1:T(8,128)S(1)} reduce(f32[4,64,64,128]{3,1,0,2:T(8,128)} %bitcast.62, f32[]{:T(128)} %constant.43.clone.1), dimensions={0}, to_apply=%region_0.0 | reduce | flops 1572864 | bytes 10485764 | tf_op jit(solution)/shard_map/reduce_sum | solution.py:81
  191.8 4.1 %collective-permute-start.4 = (bf16[32,64,128]{2,1,0:T(8,128)(2,1)}, bf16[32,64,128]{2,1,0:T(8,128)(2,1)}, u32[]{:S(2)}, u32[]{:S(2)}) collective-permute-start(bf16[32,64,128]{2,1,0:T(8,128)(2,1)} %get-tuple-element.12), channel_id=1, source_target_pairs={{0,1},{1,2},{2,3},{3,4},{4,5},{5,6},{6,7},{8,9},{9,10},{10,11},{11... | collective-permute-start | bytes 1572872 | tf_op jit(solution)/shard_map/ppermute | solution.py:17
  197.4 3.1 %fusion.31 = f32[64,128,64]{1,2,0:T(8,128)} fusion(bf16[64,64,64]{2,1,0:T(8,128)(2,1)} %param.18, f32[64,128,64]{1,2,0:T(8,128)S(1)} %fusion.26), kind=kOutput, calls=%fused_computation.39 | convolution fusion | flops 68157440 | bytes 4718592 | tf_op jit(solution)/shard_map/nab,nbk->nak/dot_general | solution.py:27
  200.5 17.8 %collective-permute-done.4 = bf16[32,64,128]{2,1,0:T(8,128)(2,1)} collective-permute-done((bf16[32,64,128]{2,1,0:T(8,128)(2,1)}, bf16[32,64,128]{2,1,0:T(8,128)(2,1)}, u32[]{:S(2)}, u32[]{:S(2)}) %collective-permute-start.4) | collective-permute-done | bytes 524320 | tf_op jit(solution)/shard_map/ppermute | solution.py:17
  219.8 13.6 %gather_fusion.3 = bf16[448,64,128]{2,1,0:T(8,128)(2,1)} fusion(bf16[128,64,128]{2,1,0:T(8,128)(2,1)S(1)} %pad_maximum_fusion.2, s32[1024]{0:T(1024)S(1)} %pad_clamp_fusion.1), kind=kCustom, calls=%fused_computation.2.clone | custom fusion | bytes 14681856 | tf_op jit(solution)/shard_map/jit(_take)/gather | solution.py:33
  233.4 10.3 %add_bitcast_fusion = f32[64,64,128]{2,1,0:T(8,128)} fusion(f32[64,128,64]{1,2,0:T(8,128)} %copy-done.2, bf16[64,64,64]{2,1,0:T(8,128)(2,1)S(1)} %copy-done.9, f32[64,128,64]{1,2,0:T(8,128)} %fusion.31, f32[64,64,128]{2,0,1:T(8,128)} %copy-done.5, bf16[64,7,64,64]{3,2,1,0:T(8,128)(2,1)} %param.20, bf16[64,7,64,128]{3,2,1,0:T(8,128)(2,1)} %bitcast.64, ...), kind=kOutput, calls=%fused_computation.31 | convolution fusion | flops 543686656 | bytes 19923392 | tf_op jit(solution)/shard_map/nab,nbk->nak/dot_general | solution.py:27
  243.7 2.3 gather_fusion
  246.0 3.3 %select_add_fusion = f32[64,64,128]{2,1,0:T(8,128)} fusion(f32[64,64,128]{2,1,0:T(8,128)} %get-tuple-element.21, f32[64,64,128]{2,1,0:T(8,128)S(1)} %gather_fusion, pred[64]{0:T(512)(128)(4,1)S(1)} %get-tuple-element.6), kind=kLoop, calls=%fused_computation.30 | loop fusion | flops 1048576 | bytes 6291520 | tf_op jit(solution)/shard_map/add | solution.py:90
  (53 shorter events, 16.0 us)
Async XLA Ops:
  6.5 1.2 copy-start
  6.5 175.3 %all-gather.3.cloned.1.call-start = ((), (), s32[]{:S(2)}) async-start(), calls=%async_computation | async-start | bytes 10485760 | tf_op jit(solution)/shard_map/all_gather | solution.py:80
  11.1 10.4 %copy-start.3 = (bf16[64,64,128]{2,1,0:T(8,128)(2,1)}, bf16[64,64,128]{2,1,0:T(8,128)(2,1)S(1)}, u32[]{:S(2)}) copy-start(bf16[64,64,128]{2,1,0:T(8,128)(2,1)S(1)} %get-tuple-element.18) | copy-start | bytes 3145732
  11.1 8.1 %copy-start.10 = (s32[64,7]{0,1:T(8,128)S(1)}, s32[64,7]{0,1:T(8,128)}, u32[]{:S(2)}) copy-start(s32[64,7]{0,1:T(8,128)} %param.16) | copy-start | bytes 5380
  11.1 8.5 %copy-start.6 = (bf16[64,64,64]{2,1,0:T(8,128)(2,1)S(1)}, bf16[64,64,64]{2,1,0:T(8,128)(2,1)}, u32[]{:S(2)}) copy-start(bf16[64,64,64]{2,1,0:T(8,128)(2,1)} %param.13) | copy-start | bytes 1572868
  12.2 27.7 %collective-permute-start = (bf16[32,64,128]{2,1,0:T(8,128)(2,1)}, bf16[32,64,128]{2,1,0:T(8,128)(2,1)}, u32[]{:S(2)}, u32[]{:S(2)}) collective-permute-start(bf16[32,64,128]{2,1,0:T(8,128)(2,1)} %get-tuple-element.16), channel_id=1, source_target_pairs={{0,1},{1,2},{2,3},{3,4},{4,5},{5,6},{6,7},{7,8},{8,9},{9,10},{10,1... | collective-permute-start | bytes 1572872 | tf_op jit(solution)/shard_map/ppermute | solution.py:17
  17.9 26.0 %collective-permute-start.1 = (bf16[32,64,128]{2,1,0:T(8,128)(2,1)}, bf16[32,64,128]{2,1,0:T(8,128)(2,1)}, u32[]{:S(2)}, u32[]{:S(2)}) collective-permute-start(bf16[32,64,128]{2,1,0:T(8,128)(2,1)} %get-tuple-element.17), channel_id=1, source_target_pairs={{1,0},{2,1},{3,2},{4,3},{5,4},{6,5},{7,6},{8,7},{9,8},{10,9},{11,1... | collective-permute-start | bytes 1572872 | tf_op jit(solution)/shard_map/ppermute | solution.py:19
  69.2 5.1 %copy-start.4 = (bf16[64,64,128]{2,1,0:T(8,128)(2,1)}, bf16[64,64,128]{2,1,0:T(8,128)(2,1)S(1)}, u32[]{:S(2)}) copy-start(bf16[64,64,128]{2,1,0:T(8,128)(2,1)S(1)} %get-tuple-element.20) | copy-start | bytes 3145732
  69.2 3.2 %copy-start.12 = (s32[64]{0:T(128)S(1)}, s32[64]{0:T(128)}, u32[]{:S(2)}) copy-start(s32[64]{0:T(128)} %param.17) | copy-start | bytes 772
  69.2 3.2 %copy-start.7 = (bf16[64,64,64]{2,1,0:T(8,128)(2,1)S(1)}, bf16[64,64,64]{2,1,0:T(8,128)(2,1)}, u32[]{:S(2)}) copy-start(bf16[64,64,64]{2,1,0:T(8,128)(2,1)} %param.13) | copy-start | bytes 1572868
  69.2 24.4 %collective-permute-start.2 = (bf16[32,64,128]{2,1,0:T(8,128)(2,1)S(1)}, bf16[32,64,128]{2,1,0:T(8,128)(2,1)S(1)}, u32[]{:S(2)}, u32[]{:S(2)}) collective-permute-start(bf16[32,64,128]{2,1,0:T(8,128)(2,1)S(1)} %get-tuple-element.14), channel_id=1, source_target_pairs={{0,1},{1,2},{2,3},{3,4},{4,5},{5,6},{6,7},{7,8},{8,9},{9,10},{10,1... | collective-permute-start | bytes 1572872 | tf_op jit(solution)/shard_map/ppermute | solution.py:17
  70.9 25.4 %collective-permute-start.3 = (bf16[32,64,128]{2,1,0:T(8,128)(2,1)S(1)}, bf16[32,64,128]{2,1,0:T(8,128)(2,1)S(1)}, u32[]{:S(2)}, u32[]{:S(2)}) collective-permute-start(bf16[32,64,128]{2,1,0:T(8,128)(2,1)S(1)} %get-tuple-element.15), channel_id=1, source_target_pairs={{1,0},{2,1},{3,2},{4,3},{5,4},{6,5},{7,6},{8,7},{9,8},{10,9},{11,1... | collective-permute-start | bytes 1572872 | tf_op jit(solution)/shard_map/ppermute | solution.py:19
  124.3 0.7 copy-start.11
  186.5 1.3 copy-start.5
  187.8 1.2 copy-start.8
  190.2 7.2 %copy-start.2 = (f32[64,128,64]{1,2,0:T(8,128)}, f32[64,128,64]{1,2,0:T(8,128)S(1)}, u32[]{:S(2)}) copy-start(f32[64,128,64]{1,2,0:T(8,128)S(1)} %fusion.26) | copy-start | bytes 6291460
  191.8 26.5 %collective-permute-start.4 = (bf16[32,64,128]{2,1,0:T(8,128)(2,1)}, bf16[32,64,128]{2,1,0:T(8,128)(2,1)}, u32[]{:S(2)}, u32[]{:S(2)}) collective-permute-start(bf16[32,64,128]{2,1,0:T(8,128)(2,1)} %get-tuple-element.12), channel_id=1, source_target_pairs={{0,1},{1,2},{2,3},{3,4},{4,5},{5,6},{6,7},{8,9},{9,10},{10,11},{11... | collective-permute-start | bytes 1572872 | tf_op jit(solution)/shard_map/ppermute | solution.py:17
  196.0 22.4 %collective-permute-start.5 = (bf16[32,64,128]{2,1,0:T(8,128)(2,1)}, bf16[32,64,128]{2,1,0:T(8,128)(2,1)}, u32[]{:S(2)}, u32[]{:S(2)}) collective-permute-start(bf16[32,64,128]{2,1,0:T(8,128)(2,1)} %get-tuple-element.13), channel_id=1, source_target_pairs={{1,0},{2,1},{3,2},{4,3},{5,4},{6,5},{7,6},{9,8},{10,9},{11,10},{12... | collective-permute-start | bytes 1572872 | tf_op jit(solution)/shard_map/ppermute | solution.py:19
  219.7 13.6 %copy-start.9 = (bf16[64,64,64]{2,1,0:T(8,128)(2,1)S(1)}, bf16[64,64,64]{2,1,0:T(8,128)(2,1)}, u32[]{:S(2)}) copy-start(bf16[64,64,64]{2,1,0:T(8,128)(2,1)} %param.19) | copy-start | bytes 1572868
  246.0 3.3 %copy-start.1 = (bf16[64,64,64]{2,1,0:T(8,128)(2,1)S(1)}, bf16[64,64,64]{2,1,0:T(8,128)(2,1)}, u32[]{:S(2)}) copy-start(bf16[64,64,64]{2,1,0:T(8,128)(2,1)} %param.14) | copy-start | bytes 1572868
Sparse Core Ops, SparseCore 0:
  124.5 57.3 all-gather.2
